TPU v7x, 32 devices: a whole 2x2x4 slice. The times are simulated.
32 devices in a mesh: league: 2 (over x), seq: 16 (over z, y, core).
Axes of the slice: x: 2, y: 2, z: 4, core: 2. Of those that a mesh axis runs over, the one named last changes fastest.
Arguments:
- queries: bfloat16 [6144, 1792], P(('league', 'seq')), parts along dimension 0, may hold values from -100 to 100
- key_rows: bfloat16 [6144, 256], P(('league', 'seq')), parts along dimension 0, may hold values from -4 to 4
- value_rows: bfloat16 [6144, 256], P(('league', 'seq')), parts along dimension 0, may hold values from -6 to 6
- residual: bfloat16 [6144, 3584], P(('league', 'seq')), parts along dimension 0, may hold values from -6 to 6
- out_weight: bfloat16 [1792, 3584], P('seq'), may hold values from -0.125 to 0.125
- norm_gain: float32 [3584], replicated, may hold values from 0.1 to 1.9
- value_head: float32 [3584], replicated, may hold values from -0.09375 to 0.09375
- valid_length: int32 [2], P('league'), parts along dimension 0, may hold values from 1537 to 3072
Outputs:
- stream: bfloat16 [6144, 3584], P(('league', 'seq')), parts along dimension 0
- values: float32 [6144], P(('league', 'seq')), parts along dimension 0
There are 2 independent parts, one for each index of `league`. A program takes and returns all parts, laid end to end along the dimension named above; an argument that names none is the same for every part. Nothing has to cross between parts.
All inputs are finite; a program needn't handle non-finite values.
Results may differ from a plain program's by a relative error of at most 0.0085.
Values may be sent and summed in bfloat16 or wider, within the bound.
A program may use at most 128 MiB of HBM per device.

v0:
```python
import math
import jax
import jax.numpy as jnp
from jax import lax
from jax.sharding import PartitionSpec as P

HEAD_DIM = 128
NEG_BIG = -1e30


def row_positions(row_index, tok_count):
    owner_dev = row_index // tok_count
    within = row_index % tok_count
    return owner_dev * tok_count + within


def attend_block(
    carried, key_block, value_block, key_pos, query_grid, query_pos, query_limit, score_scale
):

    def run_block(carry_in):
        running_max, running_sum, running_out = carry_in
        scores = (
            jnp.einsum("qgrd,kgd->qgrk", query_grid, key_block, preferred_element_type=jnp.float32)
            * score_scale
        )
        allowed = key_pos[None, None, None, :] <= query_pos[:, None, None, None]
        new_max = jnp.maximum(running_max, jnp.max(jnp.where(allowed, scores, NEG_BIG), axis=-1))
        shrink = jnp.exp(running_max - new_max)
        weights = jnp.where(allowed, jnp.exp(scores - new_max[..., None]), 0.0)
        running_sum = running_sum * shrink + jnp.sum(weights, axis=-1)
        running_out = running_out * shrink[..., None] + jnp.einsum(
            "qgrk,kgd->qgrd",
            weights.astype(jnp.bfloat16),
            value_block,
            preferred_element_type=jnp.float32,
        )
        return (new_max, running_sum, running_out)

    def keep_block(carry_in):
        return carry_in

    needed = jnp.min(key_pos) <= query_limit
    return lax.cond(needed, run_block, keep_block, carried)


def attend_piece(
    carried, key_piece, value_piece, key_pos, query_grid, query_pos, query_limit, score_scale
):
    piece_rows = key_piece.shape[0]
    block_rows = math.gcd(piece_rows, 512)
    block_count = piece_rows // block_rows
    groups = key_piece.shape[1] // HEAD_DIM
    key_blocks = key_piece.reshape(block_count, block_rows, groups, HEAD_DIM)
    value_blocks = value_piece.reshape(block_count, block_rows, groups, HEAD_DIM)
    pos_blocks = key_pos.reshape(block_count, block_rows)

    def one_block(carry_in, inputs):
        return (
            attend_block(
                carry_in,
                inputs[0],
                inputs[1],
                inputs[2],
                query_grid,
                query_pos,
                query_limit,
                score_scale,
            ),
            None,
        )

    carried, unused = lax.scan(one_block, carried, (key_blocks, value_blocks, pos_blocks))
    return carried


def per_device(
    queries, key_rows, value_rows, residual, out_weight, norm_gain, value_head, valid_length
):
    device = lax.axis_index("seq")
    tok_count = queries.shape[0]
    valid_upto = valid_length[0]
    groups = key_rows.shape[1] // HEAD_DIM
    repeats = queries.shape[1] // key_rows.shape[1]
    score_scale = HEAD_DIM ** (-0.5)
    local_rows = jnp.arange(tok_count, dtype=jnp.int32)
    query_pos = row_positions(device * tok_count + local_rows, tok_count)
    query_ok = query_pos < valid_upto
    query_limit = jnp.max(jnp.where(query_ok, query_pos, -1))
    query_grid = queries.reshape(tok_count, groups, repeats, HEAD_DIM)
    start_state = (
        jnp.full((tok_count, groups, repeats), NEG_BIG, jnp.float32),
        jnp.zeros((tok_count, groups, repeats), jnp.float32),
        jnp.zeros((tok_count, groups, repeats, HEAD_DIM), jnp.float32),
    )
    key_piece = lax.all_gather(key_rows, "seq", axis=0, tiled=True)
    key_pos = row_positions(jnp.arange(key_piece.shape[0], dtype=jnp.int32), tok_count)
    carried = attend_piece(
        start_state,
        key_piece,
        lax.all_gather(value_rows, "seq", axis=0, tiled=True),
        key_pos,
        query_grid,
        query_pos,
        query_limit,
        score_scale,
    )
    running_max, running_sum, running_out = carried
    safe_sum = jnp.where(query_ok[:, None, None], running_sum, 1.0)
    attended = jnp.where(query_ok[:, None, None, None], running_out / safe_sum[..., None], 0.0)
    attended = attended.reshape(tok_count, groups * repeats * HEAD_DIM).astype(jnp.bfloat16)
    whole_weight = lax.all_gather(out_weight, "seq", axis=0, tiled=True)
    projected = jnp.dot(attended, whole_weight, preferred_element_type=jnp.float32)
    stream = (residual.astype(jnp.float32) + projected).astype(jnp.bfloat16)
    widened = stream.astype(jnp.float32)
    normed = widened * lax.rsqrt(jnp.mean(widened * widened, axis=-1, keepdims=True) + 1e-06)
    scored = jnp.sum(normed * (norm_gain * value_head)[None, :], axis=-1)
    natural_pos = device * tok_count + local_rows
    scored = jnp.where(natural_pos < valid_upto, scored, 0.0)
    return (stream, scored)


def solution(mesh):
    placed = (
        P(("league", "seq"), None),
        P(("league", "seq"), None),
        P(("league", "seq"), None),
        P(("league", "seq"), None),
        P("seq", None),
        P(),
        P(),
        P("league"),
    )
    return jax.shard_map(
        per_device,
        mesh=mesh,
        in_specs=placed,
        out_specs=(P(("league", "seq"), None), P(("league", "seq"))),
        check_vma=False,
    )
```

profile of v0, /device:TPU:0, one launch (start us, length us, event | category | flops | bytes accessed | tf_op | source)
XLA Modules:
  0.0 211.8 jit_solution(4323758560684722332)
XLA Ops:
  7.2 0.0 copy-start.1
  7.2 0.0 copy-start.2
  7.2 0.0 all-gather.4.cloned.1.call-start
  7.2 0.7 all-gather.4.cloned.1.call-update
  7.9 0.0 all-gather.6.cloned.1.call-start
  8.0 0.7 all-gather.6.cloned.1.call-update
  8.7 0.0 all-gather.8.cloned.1.call-start
  8.7 0.7 all-gather.8.cloned.1.call-update
  10.1 1.9 reshape.101
  12.0 0.2 copy.11
  12.2 0.0 copy-done.1
  12.2 0.0 copy-done.2
  12.2 0.6 select_reduce_fusion
  12.9 39.7 %all-gather.4.cloned.1.call-done = bf16[3072,256]{1,0:T(8,128)(2,1)} async-done(((bf16[192,256]{1,0:T(8,128)(2,1)}), bf16[3072,256]{1,0:T(8,128)(2,1)}) %all-gather.4.cloned.1.call-update) | async-done | bytes 1572880 | tf_op jit(solution)/shard_map/all_gather | solution.py:96
  52.6 2.4 %reshape.100 = bf16[6,512,2,128]{3,2,1,0:T(2,128)(2,1)S(1)} reshape(bf16[3072,256]{1,0:T(8,128)(2,1)} %all-gather.4.cloned.1.call-done) | data formatting | bytes 3145728 | tf_op jit(solution)/shard_map/reshape | solution.py:54
  55.0 1.4 copy.10
  56.4 36.8 %all-gather.6.cloned.1.call-done = bf16[3072,256]{1,0:T(8,128)(2,1)} async-done(((bf16[192,256]{1,0:T(8,128)(2,1)}), bf16[3072,256]{1,0:T(8,128)(2,1)}) %all-gather.6.cloned.1.call-update) | async-done | bytes 1572880 | tf_op jit(solution)/shard_map/all_gather | solution.py:101
  93.3 2.4 %reshape.102 = bf16[6,512,2,128]{3,2,1,0:T(2,128)(2,1)S(1)} reshape(bf16[3072,256]{1,0:T(8,128)(2,1)} %all-gather.6.cloned.1.call-done) | data formatting | bytes 3145728 | tf_op jit(solution)/shard_map/reshape | solution.py:55
  95.6 1.4 copy.12
  97.0 0.1 broadcast_in_dim.74
  97.2 19.7 %while.15 = (s32[]{:T(128)}, f32[192,2,7]{0,2,1:T(8,128)S(1)}, f32[192,2,7]{0,2,1:T(8,128)S(1)}, f32[192,2,7,128]{3,0,2,1:T(8,128)S(1)}, s32[6,512]{1,0:T(8,128)...) while((s32[]{:T(128)}, f32[192,2,7]{0,2,1:T(8,128)S(1)}, ...), condition=%wide.region_7.8_spmd.clone, body=%wide.region_1.7_spmd.clone.sunk | while | flops 720577664 | bytes 21064692 | solution.py:73
  97.2 0.7 fusion.52
  99.3 6.9 %conditional.3 = ((f32[192,2,7]{0,2,1:T(8,128)S(1)}, f32[192,2,7]{0,2,1:T(8,128)S(1)}, f32[192,2,7,128]{3,0,2,1:T(8,128)S(1)})) conditional(s32[]{:T(128)} %convert_element_type.48, (f32[192,2,7]{0,2,1:T(8,128)S(1)}, f32[192,2,7]{0,2,1:T(8,128)S(1)}, f32[192,2,7,128]{3,0,2,1:T(8,128)S(1)}) %tuple.53, (s32[1,512]{1,0:T(1,128)S(1)}, ...), branch_computations={%region_3.3_spmd, %region_4.6_spmd.clone} | conditional | flops 720575808 | bytes 21056228 | solution.py:44
  99.3 0.1 broadcast_compare_fusion
  99.5 2.0 fusion.2
  101.5 1.8 fusion.6
  103.3 2.9 %fusion.16 = f32[192,2,7,128]{3,0,2,1:T(8,128)S(1)} fusion(f32[2,512,192,7]{1,2,3,0:T(8,128)S(1)} %get-tuple-element.265, f32[192,2,7]{0,2,1:T(8,128)S(1)} %max.5, pred[192,512]{1,0:T(8,128)(4,1)S(1)} %broadcast_compare_fusion, f32[192,2,7,128]{3,0,2,1:T(8,128)S(1)} %get-tuple-element.208, f32[192,2,7]{0,2,1:T(8,128)S(1)} %get-tuple-element.261, ...), kind=kOutput, calls=%fused_computation.14 | convolution fusion | flops 358514688 | bytes 8640000 | tf_op jit(solution)/shard_map/while/body/eval_jaxpr/cond/branch_1_fun/qgrk,kgd->qgrd/dot_general | solution.py:32
  106.2 0.7 fusion.52
  108.3 0.7 fusion.52
  110.5 0.7 fusion.52
  112.6 0.7 fusion.52
  114.8 0.7 fusion.52
  116.9 0.5 select_convert_fusion
  117.4 0.5 copy.13
  117.9 0.7 convert_element_type.25
  118.6 77.7 %all-gather.8.cloned.1.call-done = bf16[1792,3584]{1,0:T(8,128)(2,1)} async-done(((bf16[112,3584]{1,0:T(8,128)(2,1)}), bf16[1792,3584]{1,0:T(8,128)(2,1)}) %all-gather.8.cloned.1.call-update) | async-done | bytes 12845072 | tf_op jit(solution)/shard_map/all_gather | solution.py:112
  196.3 7.8 %fusion.35 = (f32[192]{0:T(256)S(1)}, bf16[192,3584]{1,0:T(8,128)(2,1)S(1)}) fusion(bf16[192,1792]{1,0:T(8,128)(2,1)S(1)} %convert_element_type.25, bf16[1792,3584]{1,0:T(8,128)(2,1)} %all-gather.8.cloned.1.call-done, bf16[192,3584]{1,0:T(8,128)(2,1)} %param.15), kind=kOutput, calls=%fused_computation.42 | convolution fusion | flops 2470379264 | bytes 16286464 | tf_op jit(solution)/shard_map/dot_general | solution.py:113
  204.1 0.0 copy-start
  204.2 0.5 fusion.37
  204.7 0.6 compare_select_fusion
  205.3 0.0 copy-done
  (46 shorter events, 0.4 us)
Async XLA Ops:
  7.2 5.0 %copy-start.1 = (f32[3584]{0:T(1024)S(1)}, f32[3584]{0:T(1024)}, u32[]{:S(2)}) copy-start(f32[3584]{0:T(1024)} %param.17) | copy-start | bytes 43012
  7.2 5.0 %copy-start.2 = (f32[3584]{0:T(1024)S(1)}, f32[3584]{0:T(1024)}, u32[]{:S(2)}) copy-start(f32[3584]{0:T(1024)} %param.18) | copy-start | bytes 43012
  7.2 45.4 %all-gather.4.cloned.1.call-start = ((), (), s32[]{:S(2)}) async-start(), calls=%async_computation | async-start | bytes 1671168 | tf_op jit(solution)/shard_map/all_gather | solution.py:96
  7.9 85.3 %all-gather.6.cloned.1.call-start = ((), (), s32[]{:S(2)}) async-start(), calls=%async_computation.1 | async-start | bytes 1671168 | tf_op jit(solution)/shard_map/all_gather | solution.py:101
  8.7 187.7 %all-gather.8.cloned.1.call-start = ((), (), s32[]{:S(2)}) async-start(), calls=%async_computation.2 | async-start | bytes 13647872 | tf_op jit(solution)/shard_map/all_gather | solution.py:112
  204.1 1.1 copy-start
Sparse Core Ops, SparseCore 0:
  10.3 42.3 all-gather.3
  54.9 38.2 all-gather.5
  95.5 100.7 all-gather.7
where the time goes:
time: 212 us
  waiting for transfers between devices  156 us (74%)
  between operations  14.6 us (7%)
  matrix products  12.7 us (6%)
  local copies, waits for them, and re-layouts  11 us (5%)
  other arithmetic  8.68 us (4%)
  loops' own time  8.39 us (4%)
    all_gather x1, waiting for transfers between devices, per_device(): whole_weight = lax.all_gather(out_weight, 'seq', axis=0, tiled=True)  77.7 us
    all_gather x1, waiting for transfers between devices, per_device(): key_piece = lax.all_gather(key_rows, 'seq', axis=0, tiled=True)  39.7 us
    all_gather x1, waiting for transfers between devices, per_device(): lax.all_gather(value_rows, 'seq', axis=0, tiled=True)  36.8 us
    another operation x1, loops' own time, attend_piece(): lax.scan(one_block, carried, (key_blocks, value_blocks, pos_blocks))  8.26 us
    dot_general x1, matrix products, per_device(): jnp.dot(attended, whole_weight, preferred_element_type=jnp.float32)  7.8 us
    reduce_min x6, other arithmetic, attend_block(): needed = jnp.min(key_pos) <= query_limit  4.3 us
  transfers between devices with their start and end apart: 3, of which 3 were waited for; matrix products, arithmetic and copies ran while one was open for 11% of the time, Pallas kernels for 0%

commit v1 on v0

--- a/solution.py
+++ b/solution.py
@@ -93,7 +93,12 @@
         jnp.zeros((tok_count, groups, repeats), jnp.float32),
         jnp.zeros((tok_count, groups, repeats, HEAD_DIM), jnp.float32),
     )
-    key_piece = lax.all_gather(key_rows, "seq", axis=0, tiled=True)
+    ring = [key_rows]
+    for hop in range(15):
+        ring.append(lax.ppermute(ring[-1], "seq", [(dev, (dev + 1) % 16) for dev in range(16)]))
+    key_piece = jnp.roll(
+        jnp.concatenate(ring[::-1], axis=0), (lax.axis_index("seq") + 1) * ring[0].shape[0], axis=0
+    )
     key_pos = row_positions(jnp.arange(key_piece.shape[0], dtype=jnp.int32), tok_count)
     carried = attend_piece(
         start_state,

time: 212 us -> 202 us (0.953)
  the two profiles are of different devices: /device:TPU:0 before, /device:TPU:31 now
where the time goes in v1:
time: 202 us; the launch traced here: 201 us
  starting transfers between devices  72.6 us (36%)
  waiting for transfers between devices  37.7 us (19%)
  matrix products  36.9 us (18%)
  other arithmetic  17.6 us (9%)
  between operations  15.1 us (7%)
  local copies, waits for them, and re-layouts  13 us (6%)
  loops' own time  7.91 us (4%)
    ppermute x15, starting transfers between devices, per_device(): lax.ppermute(ring[-1], 'seq', [(dev, (dev + 1) % 16) for dev in range(16)])  72.5 us
    ppermute x15, waiting for transfers between devices, per_device(): lax.ppermute(ring[-1], 'seq', [(dev, (dev + 1) % 16) for dev in range(16)])  36.3 us
    dot_general x6, matrix products, run_block(): jnp.einsum('qgrk,kgd->qgrd', weights.astype(jnp.bfloat16), value_block, p...  16.9 us
    dot_general x6, matrix products, run_block(): jnp.einsum('qgrd,kgd->qgrk', query_grid, key_block, preferred_element_typ...  12.2 us
    reduce_sum x6, other arithmetic, run_block(): running_sum = running_sum * shrink + jnp.sum(weights, axis=-1)  10.6 us
    dot_general x1, matrix products, per_device(): jnp.dot(attended, whole_weight, preferred_element_type=jnp.float32)  7.8 us
    another operation x1, loops' own time, attend_piece(): lax.scan(one_block, carried, (key_blocks, value_blocks, pos_blocks))  7.54 us
  transfers between devices with their start and end apart: 17, of which 14 were waited for; matrix products, arithmetic and copies ran while one was open for 29% of the time, Pallas kernels for 0%

profile of v1, /device:TPU:31, one launch (start us, length us, event | category | flops | bytes accessed | tf_op | source)
XLA Modules:
  0.0 200.9 jit_solution(17054682914979691447)
XLA Ops:
  9.2 2.0 collective-permute-done
  11.1 5.0 %collective-permute-start.1 = (bf16[192,256]{1,0:T(8,128)(2,1)S(1)}, bf16[192,256]{1,0:T(8,128)(2,1)S(1)}, u32[]{:S(2)}, u32[]{:S(2)}) collective-permute-start(bf16[192,256]{1,0:T(8,128)(2,1)S(1)} %collective-permute-done), channel_id=1, source_target_pairs={{0,1},{1,2},{2,3},{3,4},{4,5},{5,6},{6,7},{7,8},{8,9},{9,10},{10,1... | collective-permute-start | bytes 294920 | tf_op jit(solution)/shard_map/ppermute | solution.py:98
  17.8 5.1 %collective-permute-start.2 = (bf16[192,256]{1,0:T(8,128)(2,1)S(1)}, bf16[192,256]{1,0:T(8,128)(2,1)S(1)}, u32[]{:S(2)}, u32[]{:S(2)}) collective-permute-start(bf16[192,256]{1,0:T(8,128)(2,1)S(1)} %collective-permute-done.1), channel_id=1, source_target_pairs={{0,1},{1,2},{2,3},{3,4},{4,5},{5,6},{6,7},{7,8},{8,9},{9,10},{10,1... | collective-permute-start | bytes 294920 | tf_op jit(solution)/shard_map/ppermute | solution.py:98
  22.9 2.0 collective-permute-done.2
  24.9 5.2 %collective-permute-start.3 = (bf16[192,256]{1,0:T(8,128)(2,1)S(1)}, bf16[192,256]{1,0:T(8,128)(2,1)S(1)}, u32[]{:S(2)}, u32[]{:S(2)}) collective-permute-start(bf16[192,256]{1,0:T(8,128)(2,1)S(1)} %collective-permute-done.2), channel_id=1, source_target_pairs={{0,1},{1,2},{2,3},{3,4},{4,5},{5,6},{6,7},{7,8},{8,9},{9,10},{10,1... | collective-permute-start | bytes 294920 | tf_op jit(solution)/shard_map/ppermute | solution.py:98
  31.7 5.1 %collective-permute-start.4 = (bf16[192,256]{1,0:T(8,128)(2,1)S(1)}, bf16[192,256]{1,0:T(8,128)(2,1)S(1)}, u32[]{:S(2)}, u32[]{:S(2)}) collective-permute-start(bf16[192,256]{1,0:T(8,128)(2,1)S(1)} %collective-permute-done.3), channel_id=1, source_target_pairs={{0,1},{1,2},{2,3},{3,4},{4,5},{5,6},{6,7},{7,8},{8,9},{9,10},{10,1... | collective-permute-start | bytes 294920 | tf_op jit(solution)/shard_map/ppermute | solution.py:98
  36.8 3.5 %collective-permute-done.4 = bf16[192,256]{1,0:T(8,128)(2,1)S(1)} collective-permute-done((bf16[192,256]{1,0:T(8,128)(2,1)S(1)}, bf16[192,256]{1,0:T(8,128)(2,1)S(1)}, u32[]{:S(2)}, u32[]{:S(2)}) %collective-permute-start.4) | collective-permute-done | bytes 98336 | tf_op jit(solution)/shard_map/ppermute | solution.py:98
  40.4 5.2 %collective-permute-start.5 = (bf16[192,256]{1,0:T(8,128)(2,1)S(1)}, bf16[192,256]{1,0:T(8,128)(2,1)S(1)}, u32[]{:S(2)}, u32[]{:S(2)}) collective-permute-start(bf16[192,256]{1,0:T(8,128)(2,1)S(1)} %collective-permute-done.4), channel_id=1, source_target_pairs={{0,1},{1,2},{2,3},{3,4},{4,5},{5,6},{6,7},{7,8},{8,9},{9,10},{10,1... | collective-permute-start | bytes 294920 | tf_op jit(solution)/shard_map/ppermute | solution.py:98
  47.2 5.2 %collective-permute-start.6 = (bf16[192,256]{1,0:T(8,128)(2,1)S(1)}, bf16[192,256]{1,0:T(8,128)(2,1)S(1)}, u32[]{:S(2)}, u32[]{:S(2)}) collective-permute-start(bf16[192,256]{1,0:T(8,128)(2,1)S(1)} %collective-permute-done.5), channel_id=1, source_target_pairs={{0,1},{1,2},{2,3},{3,4},{4,5},{5,6},{6,7},{7,8},{8,9},{9,10},{10,1... | collective-permute-start | bytes 294920 | tf_op jit(solution)/shard_map/ppermute | solution.py:98
  54.1 5.1 %collective-permute-start.7 = (bf16[192,256]{1,0:T(8,128)(2,1)S(1)}, bf16[192,256]{1,0:T(8,128)(2,1)S(1)}, u32[]{:S(2)}, u32[]{:S(2)}) collective-permute-start(bf16[192,256]{1,0:T(8,128)(2,1)S(1)} %collective-permute-done.6), channel_id=1, source_target_pairs={{0,1},{1,2},{2,3},{3,4},{4,5},{5,6},{6,7},{7,8},{8,9},{9,10},{10,1... | collective-permute-start | bytes 294920 | tf_op jit(solution)/shard_map/ppermute | solution.py:98
  60.8 5.2 %collective-permute-start.8 = (bf16[192,256]{1,0:T(8,128)(2,1)S(1)}, bf16[192,256]{1,0:T(8,128)(2,1)S(1)}, u32[]{:S(2)}, u32[]{:S(2)}) collective-permute-start(bf16[192,256]{1,0:T(8,128)(2,1)S(1)} %collective-permute-done.7), channel_id=1, source_target_pairs={{0,1},{1,2},{2,3},{3,4},{4,5},{5,6},{6,7},{7,8},{8,9},{9,10},{10,1... | collective-permute-start | bytes 294920 | tf_op jit(solution)/shard_map/ppermute | solution.py:98
  66.0 3.8 %collective-permute-done.8 = bf16[192,256]{1,0:T(8,128)(2,1)S(1)} collective-permute-done((bf16[192,256]{1,0:T(8,128)(2,1)S(1)}, bf16[192,256]{1,0:T(8,128)(2,1)S(1)}, u32[]{:S(2)}, u32[]{:S(2)}) %collective-permute-start.8) | collective-permute-done | bytes 98336 | tf_op jit(solution)/shard_map/ppermute | solution.py:98
  69.8 5.2 %collective-permute-start.9 = (bf16[192,256]{1,0:T(8,128)(2,1)S(1)}, bf16[192,256]{1,0:T(8,128)(2,1)S(1)}, u32[]{:S(2)}, u32[]{:S(2)}) collective-permute-start(bf16[192,256]{1,0:T(8,128)(2,1)S(1)} %collective-permute-done.8), channel_id=1, source_target_pairs={{0,1},{1,2},{2,3},{3,4},{4,5},{5,6},{6,7},{7,8},{8,9},{9,10},{10,1... | collective-permute-start | bytes 294920 | tf_op jit(solution)/shard_map/ppermute | solution.py:98
  75.0 3.8 %collective-permute-done.9 = bf16[192,256]{1,0:T(8,128)(2,1)S(1)} collective-permute-done((bf16[192,256]{1,0:T(8,128)(2,1)S(1)}, bf16[192,256]{1,0:T(8,128)(2,1)S(1)}, u32[]{:S(2)}, u32[]{:S(2)}) %collective-permute-start.9) | collective-permute-done | bytes 98336 | tf_op jit(solution)/shard_map/ppermute | solution.py:98
  78.8 5.2 %collective-permute-start.10 = (bf16[192,256]{1,0:T(8,128)(2,1)S(1)}, bf16[192,256]{1,0:T(8,128)(2,1)S(1)}, u32[]{:S(2)}, u32[]{:S(2)}) collective-permute-start(bf16[192,256]{1,0:T(8,128)(2,1)S(1)} %collective-permute-done.9), channel_id=1, source_target_pairs={{0,1},{1,2},{2,3},{3,4},{4,5},{5,6},{6,7},{7,8},{8,9},{9,10},{10,1... | collective-permute-start | bytes 294920 | tf_op jit(solution)/shard_map/ppermute | solution.py:98
  83.9 3.8 %collective-permute-done.10 = bf16[192,256]{1,0:T(8,128)(2,1)S(1)} collective-permute-done((bf16[192,256]{1,0:T(8,128)(2,1)S(1)}, bf16[192,256]{1,0:T(8,128)(2,1)S(1)}, u32[]{:S(2)}, u32[]{:S(2)}) %collective-permute-start.10) | collective-permute-done | bytes 98336 | tf_op jit(solution)/shard_map/ppermute | solution.py:98
  87.7 5.2 %collective-permute-start.11 = (bf16[192,256]{1,0:T(8,128)(2,1)S(1)}, bf16[192,256]{1,0:T(8,128)(2,1)S(1)}, u32[]{:S(2)}, u32[]{:S(2)}) collective-permute-start(bf16[192,256]{1,0:T(8,128)(2,1)S(1)} %collective-permute-done.10), channel_id=1, source_target_pairs={{0,1},{1,2},{2,3},{3,4},{4,5},{5,6},{6,7},{7,8},{8,9},{9,10},{10,1... | collective-permute-start | bytes 294920 | tf_op jit(solution)/shard_map/ppermute | solution.py:98
  94.6 5.1 %collective-permute-start.12 = (bf16[192,256]{1,0:T(8,128)(2,1)S(1)}, bf16[192,256]{1,0:T(8,128)(2,1)S(1)}, u32[]{:S(2)}, u32[]{:S(2)}) collective-permute-start(bf16[192,256]{1,0:T(8,128)(2,1)S(1)} %collective-permute-done.11), channel_id=1, source_target_pairs={{0,1},{1,2},{2,3},{3,4},{4,5},{5,6},{6,7},{7,8},{8,9},{9,10},{10,1... | collective-permute-start | bytes 294920 | tf_op jit(solution)/shard_map/ppermute | solution.py:98
  100.3 2.1 %reshape.101 = bf16[192,2,7,128]{3,2,1,0:T(8,128)(2,1)S(1)} reshape(bf16[192,1792]{1,0:T(8,128)(2,1)} %param.12) | data formatting | bytes 1376256 | tf_op jit(solution)/shard_map/reshape | solution.py:90
  103.3 5.2 %collective-permute-start.13 = (bf16[192,256]{1,0:T(8,128)(2,1)S(1)}, bf16[192,256]{1,0:T(8,128)(2,1)S(1)}, u32[]{:S(2)}, u32[]{:S(2)}) collective-permute-start(bf16[192,256]{1,0:T(8,128)(2,1)S(1)} %collective-permute-done.12), channel_id=1, source_target_pairs={{0,1},{1,2},{2,3},{3,4},{4,5},{5,6},{6,7},{7,8},{8,9},{9,10},{10,1... | collective-permute-start | bytes 294920 | tf_op jit(solution)/shard_map/ppermute | solution.py:98
  108.5 3.8 %collective-permute-done.13 = bf16[192,256]{1,0:T(8,128)(2,1)S(1)} collective-permute-done((bf16[192,256]{1,0:T(8,128)(2,1)S(1)}, bf16[192,256]{1,0:T(8,128)(2,1)S(1)}, u32[]{:S(2)}, u32[]{:S(2)}) %collective-permute-start.13) | collective-permute-done | bytes 98336 | tf_op jit(solution)/shard_map/ppermute | solution.py:98
  112.2 5.2 %collective-permute-start.14 = (bf16[192,256]{1,0:T(8,128)(2,1)S(1)}, bf16[192,256]{1,0:T(8,128)(2,1)S(1)}, u32[]{:S(2)}, u32[]{:S(2)}) collective-permute-start(bf16[192,256]{1,0:T(8,128)(2,1)S(1)} %collective-permute-done.13), channel_id=1, source_target_pairs={{0,1},{1,2},{2,3},{3,4},{4,5},{5,6},{6,7},{7,8},{8,9},{9,10},{10,1... | collective-permute-start | bytes 294920 | tf_op jit(solution)/shard_map/ppermute | solution.py:98
  117.4 3.8 %collective-permute-done.14 = bf16[192,256]{1,0:T(8,128)(2,1)S(1)} collective-permute-done((bf16[192,256]{1,0:T(8,128)(2,1)S(1)}, bf16[192,256]{1,0:T(8,128)(2,1)S(1)}, u32[]{:S(2)}, u32[]{:S(2)}) %collective-permute-start.14) | collective-permute-done | bytes 98336 | tf_op jit(solution)/shard_map/ppermute | solution.py:98
  123.3 2.4 %reshape.100 = bf16[6,512,2,128]{3,2,1,0:T(2,128)(2,1)S(1)} reshape(bf16[3072,256]{1,0:T(8,128)(2,1)} %constant_dynamic-slice_fusion.1) | data formatting | bytes 3145728 | tf_op jit(solution)/shard_map/reshape | solution.py:54
  127.1 2.4 %reshape.102 = bf16[6,512,2,128]{3,2,1,0:T(2,128)(2,1)S(1)} reshape(bf16[3072,256]{1,0:T(8,128)(2,1)} %all-gather.3.cloned.1.call-done) | data formatting | bytes 3145728 | tf_op jit(solution)/shard_map/reshape | solution.py:55
  131.0 52.4 %while.15 = (s32[]{:T(128)}, f32[192,2,7]{0,2,1:T(8,128)S(1)}, f32[192,2,7]{0,2,1:T(8,128)S(1)}, f32[192,2,7,128]{3,0,2,1:T(8,128)S(1)}, s32[6,512]{1,0:T(8,128)...) while((s32[]{:T(128)}, f32[192,2,7]{0,2,1:T(8,128)S(1)}, ...), condition=%wide.region_7.8_spmd.clone, body=%wide.region_1.7_spmd.clone.sunk | while | flops 720577664 | bytes 21064692 | solution.py:73
  132.9 6.8 %conditional.3 = ((f32[192,2,7]{0,2,1:T(8,128)S(1)}, f32[192,2,7]{0,2,1:T(8,128)S(1)}, f32[192,2,7,128]{3,0,2,1:T(8,128)S(1)})) conditional(s32[]{:T(128)} %convert_element_type.48, (f32[192,2,7]{0,2,1:T(8,128)S(1)}, f32[192,2,7]{0,2,1:T(8,128)S(1)}, f32[192,2,7,128]{3,0,2,1:T(8,128)S(1)}) %tuple.53, (s32[1,512]{1,0:T(1,128)S(1)}, ...), branch_computations={%region_3.3_spmd, %region_4.6_spmd.clone} | conditional | flops 720575808 | bytes 21056228 | solution.py:44
  133.1 2.0 %fusion.2 = (f32[192,2,7]{0,2,1:T(8,128)S(1)}, f32[2,512,192,7]{1,2,3,0:T(8,128)S(1)}) fusion(pred[192,512]{1,0:T(8,128)(4,1)S(1)} %broadcast_compare_fusion, bf16[192,2,7,128]{3,0,2,1:T(8,128)(2,1)S(1)} %get-tuple-element.206, bf16[6,512,2,128]{3,1,2,0:T(8,128)(2,1)} %get-tuple-element.204, s32[]{:T(128)} %get-tuple-element.205), kind=kOutput, calls=%fused_computation.3 | convolution fusion | flops 356447616 | bytes 6564864 | tf_op jit(solution)/shard_map/while/body/eval_jaxpr/cond/branch_1_fun/qgrd,kgd->qgrk/dot_general | solution.py:24
  136.9 2.8 %fusion.16 = f32[192,2,7,128]{3,0,2,1:T(8,128)S(1)} fusion(f32[2,512,192,7]{1,2,3,0:T(8,128)S(1)} %get-tuple-element.265, f32[192,2,7]{0,2,1:T(8,128)S(1)} %max.5, pred[192,512]{1,0:T(8,128)(4,1)S(1)} %broadcast_compare_fusion, f32[192,2,7,128]{3,0,2,1:T(8,128)S(1)} %get-tuple-element.208, f32[192,2,7]{0,2,1:T(8,128)S(1)} %get-tuple-element.261, ...), kind=kOutput, calls=%fused_computation.14 | convolution fusion | flops 358514688 | bytes 8640000 | tf_op jit(solution)/shard_map/while/body/eval_jaxpr/cond/branch_1_fun/qgrk,kgd->qgrd/dot_general | solution.py:32
  141.6 6.8 %conditional.3 = ((f32[192,2,7]{0,2,1:T(8,128)S(1)}, f32[192,2,7]{0,2,1:T(8,128)S(1)}, f32[192,2,7,128]{3,0,2,1:T(8,128)S(1)})) conditional(s32[]{:T(128)} %convert_element_type.48, (f32[192,2,7]{0,2,1:T(8,128)S(1)}, f32[192,2,7]{0,2,1:T(8,128)S(1)}, f32[192,2,7,128]{3,0,2,1:T(8,128)S(1)}) %tuple.53, (s32[1,512]{1,0:T(1,128)S(1)}, ...), branch_computations={%region_3.3_spmd, %region_4.6_spmd.clone} | conditional | flops 720575808 | bytes 21056228 | solution.py:44
  141.8 2.0 %fusion.2 = (f32[192,2,7]{0,2,1:T(8,128)S(1)}, f32[2,512,192,7]{1,2,3,0:T(8,128)S(1)}) fusion(pred[192,512]{1,0:T(8,128)(4,1)S(1)} %broadcast_compare_fusion, bf16[192,2,7,128]{3,0,2,1:T(8,128)(2,1)S(1)} %get-tuple-element.206, bf16[6,512,2,128]{3,1,2,0:T(8,128)(2,1)} %get-tuple-element.204, s32[]{:T(128)} %get-tuple-element.205), kind=kOutput, calls=%fused_computation.3 | convolution fusion | flops 356447616 | bytes 6564864 | tf_op jit(solution)/shard_map/while/body/eval_jaxpr/cond/branch_1_fun/qgrd,kgd->qgrk/dot_general | solution.py:24
  143.8 1.8 fusion.6
  145.6 2.8 %fusion.16 = f32[192,2,7,128]{3,0,2,1:T(8,128)S(1)} fusion(f32[2,512,192,7]{1,2,3,0:T(8,128)S(1)} %get-tuple-element.265, f32[192,2,7]{0,2,1:T(8,128)S(1)} %max.5, pred[192,512]{1,0:T(8,128)(4,1)S(1)} %broadcast_compare_fusion, f32[192,2,7,128]{3,0,2,1:T(8,128)S(1)} %get-tuple-element.208, f32[192,2,7]{0,2,1:T(8,128)S(1)} %get-tuple-element.261, ...), kind=kOutput, calls=%fused_computation.14 | convolution fusion | flops 358514688 | bytes 8640000 | tf_op jit(solution)/shard_map/while/body/eval_jaxpr/cond/branch_1_fun/qgrk,kgd->qgrd/dot_general | solution.py:32
  150.3 6.9 %conditional.3 = ((f32[192,2,7]{0,2,1:T(8,128)S(1)}, f32[192,2,7]{0,2,1:T(8,128)S(1)}, f32[192,2,7,128]{3,0,2,1:T(8,128)S(1)})) conditional(s32[]{:T(128)} %convert_element_type.48, (f32[192,2,7]{0,2,1:T(8,128)S(1)}, f32[192,2,7]{0,2,1:T(8,128)S(1)}, f32[192,2,7,128]{3,0,2,1:T(8,128)S(1)}) %tuple.53, (s32[1,512]{1,0:T(1,128)S(1)}, ...), branch_computations={%region_3.3_spmd, %region_4.6_spmd.clone} | conditional | flops 720575808 | bytes 21056228 | solution.py:44
  150.5 2.1 %fusion.2 = (f32[192,2,7]{0,2,1:T(8,128)S(1)}, f32[2,512,192,7]{1,2,3,0:T(8,128)S(1)}) fusion(pred[192,512]{1,0:T(8,128)(4,1)S(1)} %broadcast_compare_fusion, bf16[192,2,7,128]{3,0,2,1:T(8,128)(2,1)S(1)} %get-tuple-element.206, bf16[6,512,2,128]{3,1,2,0:T(8,128)(2,1)} %get-tuple-element.204, s32[]{:T(128)} %get-tuple-element.205), kind=kOutput, calls=%fused_computation.3 | convolution fusion | flops 356447616 | bytes 6564864 | tf_op jit(solution)/shard_map/while/body/eval_jaxpr/cond/branch_1_fun/qgrd,kgd->qgrk/dot_general | solution.py:24
  152.6 1.8 fusion.6
  154.4 2.8 %fusion.16 = f32[192,2,7,128]{3,0,2,1:T(8,128)S(1)} fusion(f32[2,512,192,7]{1,2,3,0:T(8,128)S(1)} %get-tuple-element.265, f32[192,2,7]{0,2,1:T(8,128)S(1)} %max.5, pred[192,512]{1,0:T(8,128)(4,1)S(1)} %broadcast_compare_fusion, f32[192,2,7,128]{3,0,2,1:T(8,128)S(1)} %get-tuple-element.208, f32[192,2,7]{0,2,1:T(8,128)S(1)} %get-tuple-element.261, ...), kind=kOutput, calls=%fused_computation.14 | convolution fusion | flops 358514688 | bytes 8640000 | tf_op jit(solution)/shard_map/while/body/eval_jaxpr/cond/branch_1_fun/qgrk,kgd->qgrd/dot_general | solution.py:32
  159.2 6.8 %conditional.3 = ((f32[192,2,7]{0,2,1:T(8,128)S(1)}, f32[192,2,7]{0,2,1:T(8,128)S(1)}, f32[192,2,7,128]{3,0,2,1:T(8,128)S(1)})) conditional(s32[]{:T(128)} %convert_element_type.48, (f32[192,2,7]{0,2,1:T(8,128)S(1)}, f32[192,2,7]{0,2,1:T(8,128)S(1)}, f32[192,2,7,128]{3,0,2,1:T(8,128)S(1)}) %tuple.53, (s32[1,512]{1,0:T(1,128)S(1)}, ...), branch_computations={%region_3.3_spmd, %region_4.6_spmd.clone} | conditional | flops 720575808 | bytes 21056228 | solution.py:44
  159.3 2.0 %fusion.2 = (f32[192,2,7]{0,2,1:T(8,128)S(1)}, f32[2,512,192,7]{1,2,3,0:T(8,128)S(1)}) fusion(pred[192,512]{1,0:T(8,128)(4,1)S(1)} %broadcast_compare_fusion, bf16[192,2,7,128]{3,0,2,1:T(8,128)(2,1)S(1)} %get-tuple-element.206, bf16[6,512,2,128]{3,1,2,0:T(8,128)(2,1)} %get-tuple-element.204, s32[]{:T(128)} %get-tuple-element.205), kind=kOutput, calls=%fused_computation.3 | convolution fusion | flops 356447616 | bytes 6564864 | tf_op jit(solution)/shard_map/while/body/eval_jaxpr/cond/branch_1_fun/qgrd,kgd->qgrk/dot_general | solution.py:24
  163.2 2.8 %fusion.16 = f32[192,2,7,128]{3,0,2,1:T(8,128)S(1)} fusion(f32[2,512,192,7]{1,2,3,0:T(8,128)S(1)} %get-tuple-element.265, f32[192,2,7]{0,2,1:T(8,128)S(1)} %max.5, pred[192,512]{1,0:T(8,128)(4,1)S(1)} %broadcast_compare_fusion, f32[192,2,7,128]{3,0,2,1:T(8,128)S(1)} %get-tuple-element.208, f32[192,2,7]{0,2,1:T(8,128)S(1)} %get-tuple-element.261, ...), kind=kOutput, calls=%fused_computation.14 | convolution fusion | flops 358514688 | bytes 8640000 | tf_op jit(solution)/shard_map/while/body/eval_jaxpr/cond/branch_1_fun/qgrk,kgd->qgrd/dot_general | solution.py:32
  167.9 6.8 %conditional.3 = ((f32[192,2,7]{0,2,1:T(8,128)S(1)}, f32[192,2,7]{0,2,1:T(8,128)S(1)}, f32[192,2,7,128]{3,0,2,1:T(8,128)S(1)})) conditional(s32[]{:T(128)} %convert_element_type.48, (f32[192,2,7]{0,2,1:T(8,128)S(1)}, f32[192,2,7]{0,2,1:T(8,128)S(1)}, f32[192,2,7,128]{3,0,2,1:T(8,128)S(1)}) %tuple.53, (s32[1,512]{1,0:T(1,128)S(1)}, ...), branch_computations={%region_3.3_spmd, %region_4.6_spmd.clone} | conditional | flops 720575808 | bytes 21056228 | solution.py:44
  168.1 2.0 %fusion.2 = (f32[192,2,7]{0,2,1:T(8,128)S(1)}, f32[2,512,192,7]{1,2,3,0:T(8,128)S(1)}) fusion(pred[192,512]{1,0:T(8,128)(4,1)S(1)} %broadcast_compare_fusion, bf16[192,2,7,128]{3,0,2,1:T(8,128)(2,1)S(1)} %get-tuple-element.206, bf16[6,512,2,128]{3,1,2,0:T(8,128)(2,1)} %get-tuple-element.204, s32[]{:T(128)} %get-tuple-element.205), kind=kOutput, calls=%fused_computation.3 | convolution fusion | flops 356447616 | bytes 6564864 | tf_op jit(solution)/shard_map/while/body/eval_jaxpr/cond/branch_1_fun/qgrd,kgd->qgrk/dot_general | solution.py:24
  170.1 1.8 fusion.6
  171.9 2.8 %fusion.16 = f32[192,2,7,128]{3,0,2,1:T(8,128)S(1)} fusion(f32[2,512,192,7]{1,2,3,0:T(8,128)S(1)} %get-tuple-element.265, f32[192,2,7]{0,2,1:T(8,128)S(1)} %max.5, pred[192,512]{1,0:T(8,128)(4,1)S(1)} %broadcast_compare_fusion, f32[192,2,7,128]{3,0,2,1:T(8,128)S(1)} %get-tuple-element.208, f32[192,2,7]{0,2,1:T(8,128)S(1)} %get-tuple-element.261, ...), kind=kOutput, calls=%fused_computation.14 | convolution fusion | flops 358514688 | bytes 8640000 | tf_op jit(solution)/shard_map/while/body/eval_jaxpr/cond/branch_1_fun/qgrk,kgd->qgrd/dot_general | solution.py:32
  176.6 6.8 %conditional.3 = ((f32[192,2,7]{0,2,1:T(8,128)S(1)}, f32[192,2,7]{0,2,1:T(8,128)S(1)}, f32[192,2,7,128]{3,0,2,1:T(8,128)S(1)})) conditional(s32[]{:T(128)} %convert_element_type.48, (f32[192,2,7]{0,2,1:T(8,128)S(1)}, f32[192,2,7]{0,2,1:T(8,128)S(1)}, f32[192,2,7,128]{3,0,2,1:T(8,128)S(1)}) %tuple.53, (s32[1,512]{1,0:T(1,128)S(1)}, ...), branch_computations={%region_3.3_spmd, %region_4.6_spmd.clone} | conditional | flops 720575808 | bytes 21056228 | solution.py:44
  176.8 2.0 %fusion.2 = (f32[192,2,7]{0,2,1:T(8,128)S(1)}, f32[2,512,192,7]{1,2,3,0:T(8,128)S(1)}) fusion(pred[192,512]{1,0:T(8,128)(4,1)S(1)} %broadcast_compare_fusion, bf16[192,2,7,128]{3,0,2,1:T(8,128)(2,1)S(1)} %get-tuple-element.206, bf16[6,512,2,128]{3,1,2,0:T(8,128)(2,1)} %get-tuple-element.204, s32[]{:T(128)} %get-tuple-element.205), kind=kOutput, calls=%fused_computation.3 | convolution fusion | flops 356447616 | bytes 6564864 | tf_op jit(solution)/shard_map/while/body/eval_jaxpr/cond/branch_1_fun/qgrd,kgd->qgrk/dot_general | solution.py:24
  180.6 2.8 %fusion.16 = f32[192,2,7,128]{3,0,2,1:T(8,128)S(1)} fusion(f32[2,512,192,7]{1,2,3,0:T(8,128)S(1)} %get-tuple-element.265, f32[192,2,7]{0,2,1:T(8,128)S(1)} %max.5, pred[192,512]{1,0:T(8,128)(4,1)S(1)} %broadcast_compare_fusion, f32[192,2,7,128]{3,0,2,1:T(8,128)S(1)} %get-tuple-element.208, f32[192,2,7]{0,2,1:T(8,128)S(1)} %get-tuple-element.261, ...), kind=kOutput, calls=%fused_computation.14 | convolution fusion | flops 358514688 | bytes 8640000 | tf_op jit(solution)/shard_map/while/body/eval_jaxpr/cond/branch_1_fun/qgrk,kgd->qgrd/dot_general | solution.py:32
  185.2 7.8 %fusion.35 = (f32[192]{0:T(256)S(1)}, bf16[192,3584]{1,0:T(8,128)(2,1)S(1)}) fusion(bf16[192,1792]{1,0:T(8,128)(2,1)S(1)} %convert_element_type.25, bf16[1792,3584]{1,0:T(8,128)(2,1)} %all-gather.5.cloned.1.call-done, bf16[192,3584]{1,0:T(8,128)(2,1)} %param.15), kind=kOutput, calls=%fused_computation.42 | convolution fusion | flops 2470379264 | bytes 16286464 | tf_op jit(solution)/shard_map/dot_general | solution.py:118
  (141 shorter events, 30.5 us)
Async XLA Ops:
  7.2 95.4 %copy-start.2 = (f32[3584]{0:T(1024)S(1)}, f32[3584]{0:T(1024)}, u32[]{:S(2)}) copy-start(f32[3584]{0:T(1024)} %param.17) | copy-start | bytes 43012
  7.2 95.4 %copy-start.3 = (f32[3584]{0:T(1024)S(1)}, f32[3584]{0:T(1024)}, u32[]{:S(2)}) copy-start(f32[3584]{0:T(1024)} %param.18) | copy-start | bytes 43012
  7.2 119.9 %all-gather.3.cloned.1.call-start = ((), (), s32[]{:S(2)}) async-start(), calls=%async_computation | async-start | bytes 1671168 | tf_op jit(solution)/shard_map/all_gather | solution.py:106
  7.9 177.2 %all-gather.5.cloned.1.call-start = ((), (), s32[]{:S(2)}) async-start(), calls=%async_computation.1 | async-start | bytes 13647872 | tf_op jit(solution)/shard_map/all_gather | solution.py:117
  8.7 112.8 %copy-start.1 = (bf16[192,256]{1,0:T(8,128)(2,1)S(1)}, bf16[192,256]{1,0:T(8,128)(2,1)}, u32[]{:S(2)}) copy-start(bf16[192,256]{1,0:T(8,128)(2,1)} %param.13) | copy-start | bytes 294916
  8.7 2.5 %collective-permute-start = (bf16[192,256]{1,0:T(8,128)(2,1)}, bf16[192,256]{1,0:T(8,128)(2,1)S(1)}, u32[]{:S(2)}, u32[]{:S(2)}) collective-permute-start(bf16[192,256]{1,0:T(8,128)(2,1)} %param.13), channel_id=1, source_target_pairs={{0,1},{1,2},{2,3},{3,4},{4,5},{5,6},{6,7},{7,8},{8,9},{9,10},{10,1... | collective-permute-start | bytes 294920 | tf_op jit(solution)/shard_map/ppermute | solution.py:98
  11.1 6.6 %collective-permute-start.1 = (bf16[192,256]{1,0:T(8,128)(2,1)S(1)}, bf16[192,256]{1,0:T(8,128)(2,1)S(1)}, u32[]{:S(2)}, u32[]{:S(2)}) collective-permute-start(bf16[192,256]{1,0:T(8,128)(2,1)S(1)} %collective-permute-done), channel_id=1, source_target_pairs={{0,1},{1,2},{2,3},{3,4},{4,5},{5,6},{6,7},{7,8},{8,9},{9,10},{10,1... | collective-permute-start | bytes 294920 | tf_op jit(solution)/shard_map/ppermute | solution.py:98
  17.8 7.1 %collective-permute-start.2 = (bf16[192,256]{1,0:T(8,128)(2,1)S(1)}, bf16[192,256]{1,0:T(8,128)(2,1)S(1)}, u32[]{:S(2)}, u32[]{:S(2)}) collective-permute-start(bf16[192,256]{1,0:T(8,128)(2,1)S(1)} %collective-permute-done.1), channel_id=1, source_target_pairs={{0,1},{1,2},{2,3},{3,4},{4,5},{5,6},{6,7},{7,8},{8,9},{9,10},{10,1... | collective-permute-start | bytes 294920 | tf_op jit(solution)/shard_map/ppermute | solution.py:98
  24.9 6.8 %collective-permute-start.3 = (bf16[192,256]{1,0:T(8,128)(2,1)S(1)}, bf16[192,256]{1,0:T(8,128)(2,1)S(1)}, u32[]{:S(2)}, u32[]{:S(2)}) collective-permute-start(bf16[192,256]{1,0:T(8,128)(2,1)S(1)} %collective-permute-done.2), channel_id=1, source_target_pairs={{0,1},{1,2},{2,3},{3,4},{4,5},{5,6},{6,7},{7,8},{8,9},{9,10},{10,1... | collective-permute-start | bytes 294920 | tf_op jit(solution)/shard_map/ppermute | solution.py:98
  31.7 8.6 %collective-permute-start.4 = (bf16[192,256]{1,0:T(8,128)(2,1)S(1)}, bf16[192,256]{1,0:T(8,128)(2,1)S(1)}, u32[]{:S(2)}, u32[]{:S(2)}) collective-permute-start(bf16[192,256]{1,0:T(8,128)(2,1)S(1)} %collective-permute-done.3), channel_id=1, source_target_pairs={{0,1},{1,2},{2,3},{3,4},{4,5},{5,6},{6,7},{7,8},{8,9},{9,10},{10,1... | collective-permute-start | bytes 294920 | tf_op jit(solution)/shard_map/ppermute | solution.py:98
  40.4 6.9 %collective-permute-start.5 = (bf16[192,256]{1,0:T(8,128)(2,1)S(1)}, bf16[192,256]{1,0:T(8,128)(2,1)S(1)}, u32[]{:S(2)}, u32[]{:S(2)}) collective-permute-start(bf16[192,256]{1,0:T(8,128)(2,1)S(1)} %collective-permute-done.4), channel_id=1, source_target_pairs={{0,1},{1,2},{2,3},{3,4},{4,5},{5,6},{6,7},{7,8},{8,9},{9,10},{10,1... | collective-permute-start | bytes 294920 | tf_op jit(solution)/shard_map/ppermute | solution.py:98
  47.2 6.8 %collective-permute-start.6 = (bf16[192,256]{1,0:T(8,128)(2,1)S(1)}, bf16[192,256]{1,0:T(8,128)(2,1)S(1)}, u32[]{:S(2)}, u32[]{:S(2)}) collective-permute-start(bf16[192,256]{1,0:T(8,128)(2,1)S(1)} %collective-permute-done.5), channel_id=1, source_target_pairs={{0,1},{1,2},{2,3},{3,4},{4,5},{5,6},{6,7},{7,8},{8,9},{9,10},{10,1... | collective-permute-start | bytes 294920 | tf_op jit(solution)/shard_map/ppermute | solution.py:98
  54.1 6.7 %collective-permute-start.7 = (bf16[192,256]{1,0:T(8,128)(2,1)S(1)}, bf16[192,256]{1,0:T(8,128)(2,1)S(1)}, u32[]{:S(2)}, u32[]{:S(2)}) collective-permute-start(bf16[192,256]{1,0:T(8,128)(2,1)S(1)} %collective-permute-done.6), channel_id=1, source_target_pairs={{0,1},{1,2},{2,3},{3,4},{4,5},{5,6},{6,7},{7,8},{8,9},{9,10},{10,1... | collective-permute-start | bytes 294920 | tf_op jit(solution)/shard_map/ppermute | solution.py:98
  60.8 9.0 %collective-permute-start.8 = (bf16[192,256]{1,0:T(8,128)(2,1)S(1)}, bf16[192,256]{1,0:T(8,128)(2,1)S(1)}, u32[]{:S(2)}, u32[]{:S(2)}) collective-permute-start(bf16[192,256]{1,0:T(8,128)(2,1)S(1)} %collective-permute-done.7), channel_id=1, source_target_pairs={{0,1},{1,2},{2,3},{3,4},{4,5},{5,6},{6,7},{7,8},{8,9},{9,10},{10,1... | collective-permute-start | bytes 294920 | tf_op jit(solution)/shard_map/ppermute | solution.py:98
  69.8 9.0 %collective-permute-start.9 = (bf16[192,256]{1,0:T(8,128)(2,1)S(1)}, bf16[192,256]{1,0:T(8,128)(2,1)S(1)}, u32[]{:S(2)}, u32[]{:S(2)}) collective-permute-start(bf16[192,256]{1,0:T(8,128)(2,1)S(1)} %collective-permute-done.8), channel_id=1, source_target_pairs={{0,1},{1,2},{2,3},{3,4},{4,5},{5,6},{6,7},{7,8},{8,9},{9,10},{10,1... | collective-permute-start | bytes 294920 | tf_op jit(solution)/shard_map/ppermute | solution.py:98
  78.8 9.0 %collective-permute-start.10 = (bf16[192,256]{1,0:T(8,128)(2,1)S(1)}, bf16[192,256]{1,0:T(8,128)(2,1)S(1)}, u32[]{:S(2)}, u32[]{:S(2)}) collective-permute-start(bf16[192,256]{1,0:T(8,128)(2,1)S(1)} %collective-permute-done.9), channel_id=1, source_target_pairs={{0,1},{1,2},{2,3},{3,4},{4,5},{5,6},{6,7},{7,8},{8,9},{9,10},{10,1... | collective-permute-start | bytes 294920 | tf_op jit(solution)/shard_map/ppermute | solution.py:98
  87.7 6.8 %collective-permute-start.11 = (bf16[192,256]{1,0:T(8,128)(2,1)S(1)}, bf16[192,256]{1,0:T(8,128)(2,1)S(1)}, u32[]{:S(2)}, u32[]{:S(2)}) collective-permute-start(bf16[192,256]{1,0:T(8,128)(2,1)S(1)} %collective-permute-done.10), channel_id=1, source_target_pairs={{0,1},{1,2},{2,3},{3,4},{4,5},{5,6},{6,7},{7,8},{8,9},{9,10},{10,1... | collective-permute-start | bytes 294920 | tf_op jit(solution)/shard_map/ppermute | solution.py:98
  94.6 8.7 %collective-permute-start.12 = (bf16[192,256]{1,0:T(8,128)(2,1)S(1)}, bf16[192,256]{1,0:T(8,128)(2,1)S(1)}, u32[]{:S(2)}, u32[]{:S(2)}) collective-permute-start(bf16[192,256]{1,0:T(8,128)(2,1)S(1)} %collective-permute-done.11), channel_id=1, source_target_pairs={{0,1},{1,2},{2,3},{3,4},{4,5},{5,6},{6,7},{7,8},{8,9},{9,10},{10,1... | collective-permute-start | bytes 294920 | tf_op jit(solution)/shard_map/ppermute | solution.py:98
  103.3 9.0 %collective-permute-start.13 = (bf16[192,256]{1,0:T(8,128)(2,1)S(1)}, bf16[192,256]{1,0:T(8,128)(2,1)S(1)}, u32[]{:S(2)}, u32[]{:S(2)}) collective-permute-start(bf16[192,256]{1,0:T(8,128)(2,1)S(1)} %collective-permute-done.12), channel_id=1, source_target_pairs={{0,1},{1,2},{2,3},{3,4},{4,5},{5,6},{6,7},{7,8},{8,9},{9,10},{10,1... | collective-permute-start | bytes 294920 | tf_op jit(solution)/shard_map/ppermute | solution.py:98
  112.2 9.0 %collective-permute-start.14 = (bf16[192,256]{1,0:T(8,128)(2,1)S(1)}, bf16[192,256]{1,0:T(8,128)(2,1)S(1)}, u32[]{:S(2)}, u32[]{:S(2)}) collective-permute-start(bf16[192,256]{1,0:T(8,128)(2,1)S(1)} %collective-permute-done.13), channel_id=1, source_target_pairs={{0,1},{1,2},{2,3},{3,4},{4,5},{5,6},{6,7},{7,8},{8,9},{9,10},{10,1... | collective-permute-start | bytes 294920 | tf_op jit(solution)/shard_map/ppermute | solution.py:98
  193.0 1.1 copy-start
Sparse Core Ops, SparseCore 0:
  10.3 39.1 all-gather.2
  51.7 104.6 all-gather.4
